TPU v7x, 32 devices: a whole 2x2x4 slice. The times are simulated.
32 devices in a mesh: azim: 16 (over z, y, core), rad: 2 (over x).
Axes of the slice: x: 2, y: 2, z: 4, core: 2. Of those that a mesh axis runs over, the one named last changes fastest.
Arguments:
- acoustic_state: float32 [5, 128, 32, 128], P(None, 'azim', 'rad'), may hold values from -6 to 6
- mean_flow: float32 [3, 32, 128], P(None, 'rad'), may hold values from -0.5 to 0.5
- sector_offset: int32 [2], replicated, may hold values from 0 to 15
- cell_shift: int32 [2, 128], P(None, 'azim'), may hold values from -3 to 0
- stencil_start: int32 [2, 128], P(None, 'azim'), may hold values from 0 to 1
- interface_fraction: float32 [2, 128], P(None, 'azim'), may hold values from 0 to 1
Outputs:
- next_state: float32 [5, 128, 32, 128], P(None, 'azim', 'rad')
All inputs are finite; a program needn't handle non-finite values.
Results may differ from a plain program's by a relative error of at most 0.00005.
Values sent between devices are 32-bit elements; how exact they have to be, the bound alone decides.
A program may use at most 64 MiB of HBM per device.

v0:
```python
import functools

import jax
import jax.numpy as jnp
from jax import lax
from jax.experimental import pallas as pl
from jax.experimental.pallas import tpu as pltpu
from jax.sharding import PartitionSpec as P

STENCIL = (0.841570125482, -0.244678631765, 0.059463584768, -0.007650904064)
STEP_SIZE = 0.2
MESH = pl.DeviceIdType.MESH
HIGHEST = lax.Precision.HIGHEST
GROUP = 4
RIM = 8
TILE = 8
HALO = 4


def dot(a, b):
    return jnp.dot(a, b, precision=HIGHEST, preferred_element_type=jnp.float32)


def iota(shape, dim):
    return lax.broadcasted_iota(jnp.int32, shape, dim)


def kernel(
    dims,
    q_hbm, flow_hbm, offset_hbm, shift_hbm, start_hbm, fraction_hbm,
    out_ref,
    flow_ref, offset_ref, shift_ref, start_ref, fraction_ref, in_sem,
    cur, azim_halo, rad_send, rad_halo, near, far_send, far, slopes, change, flow_pack, wide, deriv,
    near_held, far_held, near_ssem, near_rsem, far_ssem, far_rsem, azim_ssem, azim_rsem, rad_ssem, rad_rsem,
):
    fields, cells, radial, lanes, steps, n_azim, n_rad = dims
    evals = 2 * steps
    n_high = n_azim // GROUP
    middle = lanes // 2
    low_lane = middle - HALO
    r_tiles = radial // TILE
    me = lax.axis_index("azim")
    rad = lax.axis_index("rad")
    high, low = me // GROUP, lax.rem(me, GROUP)
    left, right = lax.rem(me + n_azim - 1, n_azim), lax.rem(me + 1, n_azim)
    near_peers = [lax.rem(high + i, n_high) for i in range(1, n_high)]
    far_peers = [lax.rem(low + i, GROUP) for i in range(1, GROUP)]

    rows = pl.ds(TILE, radial)
    state_in = pltpu.make_async_copy(q_hbm, cur.at[0, :, :, rows, :], in_sem.at[0])
    state_in.start()
    barrier = pltpu.get_barrier_semaphore()

    def greet(azim_to, rad_to):
        pl.semaphore_signal(barrier, inc=1, device_id=(azim_to, rad_to), device_id_type=MESH)

    for peer in near_peers:
        greet(peer * GROUP + low, rad)
    for peer in far_peers:
        greet(high * GROUP + peer, rad)
    greet(left, rad)
    greet(right, rad)

    @pl.when(rad > 0)
    def _():
        greet(me, rad - 1)

    @pl.when(rad < n_rad - 1)
    def _():
        greet(me, rad + 1)

    small_in = [
        pltpu.make_async_copy(source, target, in_sem.at[1 + i])
        for i, (source, target) in enumerate((
            (flow_hbm, flow_ref), (offset_hbm, offset_ref), (shift_hbm, shift_ref),
            (start_hbm, start_ref), (fraction_hbm, fraction_ref),
        ))
    ]
    for copy in small_in:
        copy.start()

    lane = iota((1, lanes), 1)
    lane_rim = lax.rem(lane, RIM)
    lane_group = lane // RIM
    rotor_side = lane_rim >= HALO
    lane_cell = lane_group // r_tiles

    def packed(piece_of):
        out = None
        for group in range(cells * r_tiles):
            piece = piece_of(group // r_tiles, group % r_tiles)
            turn = (RIM * group - low_lane) % lanes
            piece = pltpu.roll(piece, turn, 1) if turn else piece
            out = piece if out is None else jnp.where(lane_group == group, piece, out)
        return out

    at_interface = (lane >= low_lane) & (lane < low_lane + RIM)

    def unpacked(value, group):
        turn = (low_lane - RIM * group) % lanes
        value = pltpu.roll(value, turn, 1) if turn else value
        return jnp.where(at_interface, value, 0.0)

    def near_copy(e, slot, peer, i):
        return pltpu.make_async_remote_copy(
            src_ref=near.at[e, high], dst_ref=near.at[e, slot],
            send_sem=near_ssem.at[e, i], recv_sem=near_rsem.at[e, slot],
            device_id=(peer * GROUP + low, rad), device_id_type=MESH,
        )

    def far_copy(e, slot, peer, i):
        return pltpu.make_async_remote_copy(
            src_ref=far_send.at[e, i], dst_ref=far.at[e, slot],
            send_sem=far_ssem.at[e, i], recv_sem=far_rsem.at[e, slot],
            device_id=(high * GROUP + peer, rad), device_id_type=MESH,
        )

    def azim_copy(e, side):
        source = cells - HALO if side == 0 else 0
        return pltpu.make_async_remote_copy(
            src_ref=cur.at[e, :, pl.ds(source, HALO), rows, :], dst_ref=azim_halo.at[e, side],
            send_sem=azim_ssem.at[e, side], recv_sem=azim_rsem.at[e, side],
            device_id=(right if side == 0 else left, rad), device_id_type=MESH,
        )

    def rad_copy(e, side):
        return pltpu.make_async_remote_copy(
            src_ref=rad_send.at[e, side], dst_ref=rad_halo.at[e, side],
            send_sem=rad_ssem.at[e, side], recv_sem=rad_rsem.at[e, side],
            device_id=(me, rad + 1 if side == 0 else rad - 1), device_id_type=MESH,
        )

    def add_change(e):
        for f in range(fields):
            value = change[f]
            for group in range(cells * r_tiles):
                a, t = group // r_tiles, group % r_tiles
                spot = pl.ds(TILE * (t + 1), TILE)
                cur[e, f, a, spot, :] += unpacked(value, group)

    def send_rims(e):
        for i, peer in enumerate(near_peers):
            near_copy(e, high, peer, i).start()

    def send_halos(e):
        for side in range(2):
            azim_copy(e, side).start()

        @pl.when(rad < n_rad - 1)
        def _():
            rad_send[e, 0] = cur[e, :, :, pl.ds(TILE + radial - HALO, HALO), :]
            rad_copy(e, 0).start()

        @pl.when(rad > 0)
        def _():
            rad_send[e, 1] = cur[e, :, :, pl.ds(TILE, HALO), :]
            rad_copy(e, 1).start()

    state_in.wait()
    for f in range(fields):
        near[0, high, f] = packed(lambda a, t: cur[0, f, a, pl.ds(TILE * (t + 1), TILE), :])
    beside = jnp.where(rad > 0, 1, 0) + jnp.where(rad < n_rad - 1, 1, 0)
    pl.semaphore_wait(barrier, n_high - 1 + GROUP - 1 + 2 + beside)

    send_rims(0)
    send_halos(0)
    @pl.when(rad == 0)
    def _():
        for e in range(evals):
            rad_halo[e, 0] = jnp.zeros(rad_halo.shape[2:], jnp.float32)

    @pl.when(rad == n_rad - 1)
    def _():
        for e in range(evals):
            rad_halo[e, 1] = jnp.zeros(rad_halo.shape[2:], jnp.float32)

    for copy in small_in:
        copy.wait()
    row_no = iota((lanes, lanes), 0)
    col_no = iota((lanes, lanes), 1)
    axial = jnp.zeros((lanes, lanes), jnp.float32)
    for j in range(4):
        axial = jnp.where(row_no - col_no == j + 1, STENCIL[j], axial)
        axial = jnp.where(col_no - row_no == j + 1, -STENCIL[j], axial)
    deriv[0] = axial
    crossing = (row_no // RIM == col_no // RIM) & (
        (lax.rem(row_no, RIM) >= HALO) != (lax.rem(col_no, RIM) >= HALO)
    )
    cross = jnp.where(crossing, axial, 0.0)
    deriv[1] = cross

    def per_lane(stator_of, rotor_of, kind):
        out = jnp.zeros((1, lanes), kind)
        for a in range(cells):
            out = jnp.where(lane_cell == a, jnp.where(rotor_side, stator_of(a), rotor_of(a)), out)
        return out

    fraction = per_lane(lambda a: fraction_ref[0, a], lambda a: fraction_ref[1, a], jnp.float32)
    up_one, down_one, down_two = fraction + 1.0, fraction - 1.0, fraction - 2.0
    weights = (
        -fraction * down_one * down_two / 6.0,
        up_one * down_one * down_two / 2.0,
        -up_one * fraction * down_two / 2.0,
        up_one * fraction * down_one / 6.0,
    )
    same = (lax.rem(row_no, RIM * r_tiles) == lax.rem(col_no, RIM * r_tiles))
    for n in range(steps):
        first = per_lane(
            lambda a: shift_ref[n, a] + start_ref[0, a] - 1 + a,
            lambda a: start_ref[1, a] - shift_ref[n, a] - 4 + a,
            jnp.int32,
        )
        for d in range(3):
            point = row_no // (RIM * r_tiles) + cells * (d - 1) - first
            blend = jnp.zeros((lanes, lanes), jnp.float32)
            for m in range(4):
                blend = jnp.where(same & (point == m), weights[m], blend)
            wide[n, d] = dot(blend, cross)

    flow_pack[...] = packed(lambda a, t: flow_ref[0, TILE * t : TILE * (t + 1), :])

    def evaluate(e, carry):
        step = e // 2
        half = lax.rem(e, 2)
        scale = jnp.where(half == 0, 0.5 * STEP_SIZE, STEP_SIZE)
        offset = offset_ref[step]
        own = near[e, high].reshape(fields * TILE, lanes)
        own_cross = dot(own, deriv[1])
        for f in range(fields):
            block = cur[e, f, :, rows, :].reshape(cells * radial, lanes)
            slopes[f] = dot(block, deriv[0]).reshape(cells, radial, lanes)

        for i, peer in enumerate(near_peers):
            near_copy(e, peer, peer, i).wait_recv()
        near_held[...] = near[e]

        def needed(by, holder, sign):
            base = by + sign * offset - 1 + 2 * n_azim
            sector = base + lax.rem(holder - lax.rem(base, GROUP) + GROUP, GROUP)
            return lax.rem(sector, n_azim) // GROUP

        def chosen(peer):
            by = high * GROUP + peer
            return jnp.where(
                rotor_side[None], near_held[needed(by, low, -1)], near_held[needed(by, low, 1)]
            )

        for i, peer in enumerate(far_peers):
            far_send[e, i] = chosen(peer)
            far_copy(e, low, peer, i).start()
        far[e, low] = chosen(low)

        for side in range(2):
            azim_copy(e, side).wait_recv()

        @pl.when(rad > 0)
        def _():
            rad_copy(e, 0).wait_recv()

        @pl.when(rad < n_rad - 1)
        def _():
            rad_copy(e, 1).wait_recv()

        cur[e, :, :, pl.ds(TILE - HALO, HALO), :] = rad_halo[e, 0]
        cur[e, :, :, pl.ds(TILE + radial, HALO), :] = rad_halo[e, 1]

        def cell_row(f, a):
            if a < 0:
                return azim_halo[e, 0, f, a + HALO]
            if a >= cells:
                return azim_halo[e, 1, f, a - cells]
            return cur[e, f, a, rows, :]

        for a in range(cells):
            along = []
            for f in range(fields):
                azim = rad_slope = None
                for j in range(4):
                    term = STENCIL[j] * (cell_row(f, a + j + 1) - cell_row(f, a - j - 1))
                    azim = term if azim is None else azim + term
                    term = STENCIL[j] * (
                        cur[e, f, a, pl.ds(TILE + j + 1, radial), :]
                        - cur[e, f, a, pl.ds(TILE - j - 1, radial), :]
                    )
                    rad_slope = term if rad_slope is None else rad_slope + term
                along.append((slopes[f, a], rad_slope, azim))
            spread = along[1][0] + along[2][1] + along[3][2]
            forcing = (spread, along[4][0], along[4][1], along[4][2], spread)
            for f in range(fields):
                advect = flow_ref[0] * along[f][0] + flow_ref[1] * along[f][1] + flow_ref[2] * along[f][2]
                cur[e + 1, f, a, rows, :] = cur[e - half, f, a, rows, :] - scale * (advect + forcing[f])

        rims = [
            packed(lambda a, t: cur[e + 1, f, a, pl.ds(TILE * (t + 1), TILE), :]) for f in range(fields)
        ]

        for i, peer in enumerate(far_peers):
            far_copy(e, peer, peer, i).wait_recv()
        far_held[...] = far[e]
        moved = None
        for d in range(3):
            stator_from = lax.rem(me - offset - 1 + d + 2 * n_azim, GROUP)
            rotor_from = lax.rem(me + offset - 1 + d + 2 * n_azim, GROUP)
            facing = jnp.where(rotor_side[None], far_held[stator_from], far_held[rotor_from])
            part = dot(facing.reshape(fields * TILE, lanes), wide[step, d])
            moved = part if moved is None else moved + part
        moved = (moved - own_cross).reshape(fields, TILE, lanes)
        forced = (moved[1], moved[4], None, None, moved[1])
        for f in range(fields):
            total = flow_pack[...] * moved[f]
            if forced[f] is not None:
                total = total + forced[f]
            delta = -scale * total
            change[f] = delta
            near[e + 1, high, f] = rims[f] + delta

        @pl.when(e + 1 < evals)
        def _():
            send_rims(e + 1)
            add_change(e + 1)
            send_halos(e + 1)

        return carry

    lax.fori_loop(0, evals, evaluate, 0)
    for f in range(fields):
        value = change[f]
        for group in range(cells * r_tiles):
            a, t = group // r_tiles, group % r_tiles
            out_ref[f, a, TILE * t : TILE * (t + 1), :] = (
                cur[evals, f, a, pl.ds(TILE * (t + 1), TILE), :] + unpacked(value, group)
            )

    def finish(e, carry):
        for i, peer in enumerate(near_peers):
            near_copy(e, high, peer, i).wait_send()
        for i, peer in enumerate(far_peers):
            far_copy(e, low, peer, i).wait_send()
        for side in range(2):
            azim_copy(e, side).wait_send()

        @pl.when(rad < n_rad - 1)
        def _():
            rad_copy(e, 0).wait_send()

        @pl.when(rad > 0)
        def _():
            rad_copy(e, 1).wait_send()

        return carry

    lax.fori_loop(0, evals, finish, 0)


def solution(mesh):
    n_azim, n_rad = mesh.shape["azim"], mesh.shape["rad"]

    def shards(acoustic_state, mean_flow, sector_offset, cell_shift, stencil_start, interface_fraction):
        fields, cells, radial, lanes = acoustic_state.shape
        steps = sector_offset.shape[0]
        evals = 2 * steps
        n_high = n_azim // GROUP
        dims = (fields, cells, radial, lanes, steps, n_azim, n_rad)
        vmem = pl.BlockSpec(memory_space=pltpu.VMEM)
        f32 = jnp.float32
        dma = pltpu.SemaphoreType.DMA
        return pl.pallas_call(
            functools.partial(kernel, dims),
            out_shape=jax.ShapeDtypeStruct(acoustic_state.shape, f32),
            in_specs=[pl.BlockSpec(memory_space=pl.ANY)] * 6,
            out_specs=vmem,
            scratch_shapes=[
                pltpu.VMEM(mean_flow.shape, f32),
                pltpu.SMEM(sector_offset.shape, jnp.int32),
                pltpu.SMEM(cell_shift.shape, jnp.int32),
                pltpu.SMEM(stencil_start.shape, jnp.int32),
                pltpu.SMEM(interface_fraction.shape, f32),
                dma((6,)),
                pltpu.VMEM((evals + 1, fields, cells, radial + 2 * TILE, lanes), f32),
                pltpu.VMEM((evals, 2, fields, HALO, radial, lanes), f32),
                pltpu.VMEM((evals, 2, fields, cells, HALO, lanes), f32),
                pltpu.VMEM((evals, 2, fields, cells, HALO, lanes), f32),
                pltpu.VMEM((evals + 1, n_high, fields, TILE, lanes), f32),
                pltpu.VMEM((evals, GROUP - 1, fields, TILE, lanes), f32),
                pltpu.VMEM((evals, GROUP, fields, TILE, lanes), f32),
                pltpu.VMEM((fields, cells, radial, lanes), f32),
                pltpu.VMEM((fields, TILE, lanes), f32),
                pltpu.VMEM((TILE, lanes), f32),
                pltpu.VMEM((steps, 3, lanes, lanes), f32),
                pltpu.VMEM((2, lanes, lanes), f32),
                pltpu.VMEM((n_high, fields, TILE, lanes), f32),
                pltpu.VMEM((GROUP, fields, TILE, lanes), f32),
                dma((evals, n_high)), dma((evals, n_high)),
                dma((evals, GROUP)), dma((evals, GROUP)),
                dma((evals, 2)), dma((evals, 2)),
                dma((evals, 2)), dma((evals, 2)),
            ],
            compiler_params=pltpu.CompilerParams(collective_id=0, has_side_effects=True),
        )(acoustic_state, mean_flow, sector_offset, cell_shift, stencil_start, interface_fraction)

    return jax.shard_map(
        shards,
        mesh=mesh,
        in_specs=(
            P(None, "azim", "rad", None),
            P(None, "rad", None),
            P(),
            P(None, "azim"),
            P(None, "azim"),
            P(None, "azim"),
        ),
        out_specs=P(None, "azim", "rad", None),
        check_vma=False,
    )
```

profile of v0, /device:TPU:0, one launch (start us, length us, event | category | flops | bytes accessed | tf_op | source)
XLA Modules:
  0.0 39.2 jit_solution(11619909924568120416)
XLA Ops:
  0.0 37.5 %shard_map.64 = f32[5,8,16,128]{3,2,1,0:T(8,128)} custom-call(f32[5,8,16,128]{3,2,1,0:T(8,128)} %q_hbm.1, f32[3,16,128]{2,1,0:T(8,128)} %flow_hbm.1, s32[2]{0:T(128)} %offset_hbm.1, s32[2,8]{1,0:T(2,128)} %shift_hbm.1, s32[2,8]{1,0:T(2,128)} %start_hbm.1, f32[2,8]{1,0:T(2,128)} %fraction_hbm.1), custom_call_target="tpu_custom_call" | custom-call | tf_op jit(solution)/shard_map/pallas_call | solution.py:367
  37.5 1.7 %copy.8 = f32[5,8,16,128]{3,2,1,0:T(8,128)} copy(f32[5,8,16,128]{3,2,1,0:T(8,128)} %shard_map.64) | data formatting | bytes 655360
where the time goes:
time: 39.4 us; the launch traced here: 39.2 us
  Pallas kernels  37.5 us (95%)
  local copies, waits for them, and re-layouts  1.72 us (4%)
    pallas_call x1, Pallas kernels, shards(): pl.pallas_call(functools.partial(kernel, dims), out_shape=jax.ShapeDtypeS...  37.5 us
    unnamed x1, local copies, waits for them, and re-layouts  1.72 us

commit v1 on v0

--- a/solution.py
+++ b/solution.py
@@ -366,7 +366,7 @@
         dma = pltpu.SemaphoreType.DMA
         return pl.pallas_call(
             functools.partial(kernel, dims),
-            out_shape=jax.ShapeDtypeStruct(acoustic_state.shape, f32),
+            out_shape=pltpu.VMEM(acoustic_state.shape, f32),
             in_specs=[pl.BlockSpec(memory_space=pl.ANY)] * 6,
             out_specs=vmem,
             scratch_shapes=[

time: 39.4 us -> 37.7 us (0.957)
  local copies, waits for them, and re-layouts: 1.72 us -> 0.73 us
  Pallas kernels: 37.5 us -> 36.8 us
    unnamed x1, local copies, waits for them, and re-layouts: 1.72 us -> 0.73 us
    pallas_call x1, Pallas kernels: 37.5 us -> 36.8 us  [shards(): pl.pallas_call(functools.partial(kernel, dims), out_shape=pltpu.VMEM(acou...]
where the time goes in v1:
time: 37.7 us; the launch traced here: 37.5 us
  Pallas kernels  36.8 us (98%)
  local copies, waits for them, and re-layouts  0.73 us (2%)
    pallas_call x1, Pallas kernels, shards(): pl.pallas_call(functools.partial(kernel, dims), out_shape=pltpu.VMEM(acou...  36.8 us

profile of v1, /device:TPU:0, one launch (start us, length us, event | category | flops | bytes accessed | tf_op | source)
XLA Modules:
  0.0 37.5 jit_solution(13280057612552446734)
XLA Ops:
  0.0 36.8 %shard_map.64 = f32[5,8,16,128]{3,2,1,0:T(8,128)S(1)} custom-call(f32[5,8,16,128]{3,2,1,0:T(8,128)} %q_hbm.1, f32[3,16,128]{2,1,0:T(8,128)} %flow_hbm.1, s32[2]{0:T(128)} %offset_hbm.1, s32[2,8]{1,0:T(2,128)} %shift_hbm.1, s32[2,8]{1,0:T(2,128)} %start_hbm.1, f32[2,8]{1,0:T(2,128)} %fraction_hbm.1), custom_call_target="tpu_custom_call" | custom-call | tf_op jit(solution)/shard_map/pallas_call | solution.py:367
  36.8 0.7 %copy.8 = f32[5,8,16,128]{3,2,1,0:T(8,128)} copy(f32[5,8,16,128]{3,2,1,0:T(8,128)S(1)} %shard_map.64) | data formatting | bytes 655360

commit v2 on v1

v2 whole, which is shorter than its diff:
```python
import functools

import jax
import jax.numpy as jnp
from jax import lax
from jax.experimental import pallas as pl
from jax.experimental.pallas import tpu as pltpu
from jax.sharding import PartitionSpec as P

STENCIL = (0.841570125482, -0.244678631765, 0.059463584768, -0.007650904064)
STEP_SIZE = 0.2
MESH = pl.DeviceIdType.MESH
HIGHEST = lax.Precision.HIGHEST
GROUP = 4
RIM = 8
TILE = 8
HALO = 4


def dot(a, b):
    return jnp.dot(a, b, precision=HIGHEST, preferred_element_type=jnp.float32)


def iota(shape, dim):
    return lax.broadcasted_iota(jnp.int32, shape, dim)


def kernel(
    dims,
    q_hbm, flow_hbm, offset_hbm, shift_hbm, start_hbm, fraction_hbm,
    out_ref,
    flow_ref, offset_ref, shift_ref, start_ref, fraction_ref, in_sem,
    raw, cur, azim_halo, rad_send, rad_halo, tile, side, near, far_send, far, slopes, flow_pack, deriv,
    near_held, far_held, par, par_send, par_far,
    near_ssem, near_rsem, far_ssem, far_rsem, azim_ssem, azim_rsem, rad_ssem, rad_rsem, side_ssem, side_rsem,
    par_ssem, par_rsem, pfar_ssem, pfar_rsem,
):
    fields, cells, radial, lanes, steps, n_azim, n_rad = dims
    evals = 2 * steps
    n_high = n_azim // GROUP
    middle = lanes // 2
    low_lane = middle - HALO
    r_tiles = radial // TILE
    span = RIM * r_tiles
    me = lax.axis_index("azim")
    rad = lax.axis_index("rad")
    high, low = me // GROUP, lax.rem(me, GROUP)
    left, right = lax.rem(me + n_azim - 1, n_azim), lax.rem(me + 1, n_azim)
    near_peers = [lax.rem(high + i, n_high) for i in range(1, n_high)]
    far_peers = [lax.rem(low + i, GROUP) for i in range(1, GROUP)]

    rows = pl.ds(TILE, radial)
    state_in = pltpu.make_async_copy(q_hbm, raw.at[0], in_sem.at[0])
    state_in.start()
    barrier = pltpu.get_barrier_semaphore()

    def greet(azim_to, rad_to):
        pl.semaphore_signal(barrier, inc=1, device_id=(azim_to, rad_to), device_id_type=MESH)

    greet(left, rad)
    greet(right, rad)
    for peer in near_peers:
        greet(peer * GROUP + low, rad)
    for peer in far_peers:
        greet(high * GROUP + peer, rad)

    @pl.when(rad > 0)
    def _():
        greet(me, rad - 1)

    @pl.when(rad < n_rad - 1)
    def _():
        greet(me, rad + 1)

    small_in = [
        pltpu.make_async_copy(source, target, in_sem.at[1 + i])
        for i, (source, target) in enumerate((
            (flow_hbm, flow_ref), (offset_hbm, offset_ref), (shift_hbm, shift_ref),
            (start_hbm, start_ref), (fraction_hbm, fraction_ref),
        ))
    ]
    for copy in small_in:
        copy.start()

    shape = (TILE, lanes)
    lane = iota(shape, 1)
    line = iota(shape, 0)
    lane_rim = lax.rem(lane, RIM)
    lane_group = lane // RIM
    rotor_side = lane_rim >= HALO
    lane_cell = lane // span
    lane_tile = lax.rem(lane_group, r_tiles)
    at_interface = (lane >= low_lane) & (lane < low_lane + RIM)

    def roll(value, turn, axis=1):
        turn = turn % value.shape[axis]
        return pltpu.roll(value, turn, axis) if turn else value

    def packed(piece_of):
        out = None
        for group in range(cells * r_tiles):
            piece = roll(piece_of(group // r_tiles, group % r_tiles), RIM * group - low_lane)
            out = piece if out is None else jnp.where(lane_group == group, piece, out)
        return out

    def near_copy(e, slot, peer, i):
        return pltpu.make_async_remote_copy(
            src_ref=near.at[e, high], dst_ref=near.at[e, slot],
            send_sem=near_ssem.at[e, i], recv_sem=near_rsem.at[e, slot],
            device_id=(peer * GROUP + low, rad), device_id_type=MESH,
        )

    def far_copy(e, slot, peer, i):
        return pltpu.make_async_remote_copy(
            src_ref=far_send.at[e, i], dst_ref=far.at[e, slot],
            send_sem=far_ssem.at[e, i], recv_sem=far_rsem.at[e, slot],
            device_id=(high * GROUP + peer, rad), device_id_type=MESH,
        )

    def par_copy(slot, peer, i):
        return pltpu.make_async_remote_copy(
            src_ref=par.at[high], dst_ref=par.at[slot],
            send_sem=par_ssem.at[i], recv_sem=par_rsem.at[slot],
            device_id=(peer * GROUP + low, rad), device_id_type=MESH,
        )

    def pfar_copy(slot, peer, i):
        return pltpu.make_async_remote_copy(
            src_ref=par_send.at[i], dst_ref=par_far.at[slot],
            send_sem=pfar_ssem.at[i], recv_sem=pfar_rsem.at[slot],
            device_id=(high * GROUP + peer, rad), device_id_type=MESH,
        )

    def azim_copy(e, side_no):
        source = cells - HALO if side_no == 0 else 0
        return pltpu.make_async_remote_copy(
            src_ref=raw.at[e, :, pl.ds(source, HALO)], dst_ref=azim_halo.at[e, side_no],
            send_sem=azim_ssem.at[e, side_no], recv_sem=azim_rsem.at[e, side_no],
            device_id=(right if side_no == 0 else left, rad), device_id_type=MESH,
        )

    def rad_copy(e, side_no):
        return pltpu.make_async_remote_copy(
            src_ref=rad_send.at[e, side_no], dst_ref=rad_halo.at[e, side_no],
            send_sem=rad_ssem.at[e, side_no], recv_sem=rad_rsem.at[e, side_no],
            device_id=(me, rad + 1 if side_no == 0 else rad - 1), device_id_type=MESH,
        )

    def side_copy(e, slot):
        target = ((right, rad), (left, rad), (me, rad + 1), (me, rad - 1))[slot]
        return pltpu.make_async_remote_copy(
            src_ref=tile.at[e], dst_ref=side.at[e, slot],
            send_sem=side_ssem.at[e, slot], recv_sem=side_rsem.at[e, slot],
            device_id=target, device_id_type=MESH,
        )

    def on_rad(up, down):
        @pl.when(rad < n_rad - 1)
        def _():
            up()

        @pl.when(rad > 0)
        def _():
            down()

    def send_near(e):
        for i, peer in enumerate(near_peers):
            near_copy(e, high, peer, i).start()

    def send_sides(e):
        side_copy(e, 0).start()
        side_copy(e, 1).start()
        on_rad(lambda: side_copy(e, 2).start(), lambda: side_copy(e, 3).start())

    def wait_sides(e):
        on_rad(lambda: side_copy(e, 3).wait_recv(), lambda: side_copy(e, 2).wait_recv())
        side_copy(e, 0).wait_recv()
        side_copy(e, 1).wait_recv()

    def send_halos(e):
        for side_no in range(2):
            azim_copy(e, side_no).start()

        def up():
            rad_send[e, 0] = raw[e, :, :, pl.ds(radial - HALO, HALO), :]
            rad_copy(e, 0).start()

        def down():
            rad_send[e, 1] = raw[e, :, :, pl.ds(0, HALO), :]
            rad_copy(e, 1).start()

        on_rad(up, down)

    state_in.wait()
    for f in range(fields):
        first_tile = packed(lambda a, t: raw[0, f, a, TILE * t : TILE * (t + 1), :])
        tile[0, f] = first_tile
        near[0, high, f] = first_tile

    for copy in small_in:
        copy.wait()

    def per_lane(on_rotor, on_stator):
        out = jnp.zeros(shape, jnp.float32)
        for a in range(cells):
            out = jnp.where(lane_cell == a, jnp.where(rotor_side, on_rotor(a), on_stator(a)), out)
        return out

    def real(value):
        return value.astype(jnp.float32)

    def stator_first(n):
        return lambda a: real(shift_ref[n, a] + start_ref[0, a] - 1)

    def rotor_first(n):
        return lambda a: real(start_ref[1, a] - shift_ref[n, a] - 4)

    stator_fraction, rotor_fraction = (lambda a: fraction_ref[0, a]), (lambda a: fraction_ref[1, a])
    held = per_lane(rotor_fraction, stator_fraction)
    for n in range(steps):
        held = jnp.where(line == n + 1, per_lane(rotor_first(n), stator_first(n)), held)
    par[high] = held

    beside = jnp.where(rad > 0, 1, 0) + jnp.where(rad < n_rad - 1, 1, 0)
    pl.semaphore_wait(barrier, n_high - 1 + GROUP - 1 + 2 + beside)

    send_near(0)
    send_sides(0)
    send_halos(0)
    for i, peer in enumerate(near_peers):
        par_copy(high, peer, i).start()

    @pl.when(rad == 0)
    def _():
        for e in range(evals):
            rad_halo[e, 0] = jnp.zeros(rad_halo.shape[2:], jnp.float32)
            side[e, 2] = jnp.zeros(side.shape[2:], jnp.float32)

    @pl.when(rad == n_rad - 1)
    def _():
        for e in range(evals):
            rad_halo[e, 1] = jnp.zeros(rad_halo.shape[2:], jnp.float32)
            side[e, 3] = jnp.zeros(side.shape[2:], jnp.float32)

    row_no = iota((lanes, lanes), 0)
    col_no = iota((lanes, lanes), 1)
    axial = jnp.zeros((lanes, lanes), jnp.float32)
    for j in range(4):
        axial = jnp.where(row_no - col_no == j + 1, STENCIL[j], axial)
        axial = jnp.where(col_no - row_no == j + 1, -STENCIL[j], axial)
    deriv[...] = axial
    for i in range(3):
        flow_pack[i] = packed(lambda a, t: flow_ref[i, TILE * t : TILE * (t + 1), :])

    def taps(fraction, first):
        up_one, down_one, down_two = fraction + 1.0, fraction - 1.0, fraction - 2.0
        weights = (
            -fraction * down_one * down_two / 6.0,
            up_one * down_one * down_two / 2.0,
            -up_one * fraction * down_two / 2.0,
            up_one * fraction * down_one / 6.0,
        )
        out = []
        for delta in range(-HALO, HALO):
            tap = jnp.zeros(shape, jnp.float32)
            for m in range(4):
                tap = jnp.where(first == float(delta - m), weights[m], tap)
            out.append(tap)
        return out

    def shifted(before, here, after, delta):
        if delta < 0:
            here = jnp.where(lane_cell >= cells + delta, before, here)
        elif delta > 0:
            here = jnp.where(lane_cell < delta, after, here)
        return roll(here, -span * delta)

    def blend(before, here, after, tap):
        out = None
        for delta in range(-HALO, HALO):
            term = tap[delta + HALO] * shifted(before, here, after, delta)
            out = term if out is None else out + term
        return out

    ahead = [jnp.where((lane_rim < HALO) & (lane_rim + j + 1 >= HALO), STENCIL[j], 0.0) for j in range(4)]
    behind = [jnp.where((lane_rim >= HALO) & (lane_rim - j - 1 < HALO), STENCIL[j], 0.0) for j in range(4)]

    def cross(value):
        out = None
        for j in range(4):
            term = ahead[j] * roll(value, -(j + 1)) - behind[j] * roll(value, j + 1)
            out = term if out is None else out + term
        return out

    def azim_slope(before, here, after):
        out = None
        for j in range(4):
            term = STENCIL[j] * (
                shifted(before, here, after, j + 1) - shifted(before, here, after, -(j + 1))
            )
            out = term if out is None else out + term
        return out

    def radial_slope(below, here, above):
        last = r_tiles - 1
        following = jnp.where(lane_tile == last, roll(above, RIM * last), roll(here, -RIM))
        leading = jnp.where(lane_tile == 0, roll(below, -RIM * last), roll(here, RIM))
        out = None
        for j in range(1, 5):
            up = roll(jnp.where(line >= j, here, following), -j, 0)
            down = roll(jnp.where(line < TILE - j, here, leading), j, 0)
            term = STENCIL[j - 1] * (up - down)
            out = term if out is None else out + term
        return out

    def across(value):
        along = [cross(value[f]) for f in range(fields)]
        forcing = (along[1], along[4], None, None, along[1])
        out = []
        for f in range(fields):
            total = flow_pack[0] * along[f]
            out.append(total if forcing[f] is None else total + forcing[f])
        return out

    def swapped(value):
        return jnp.where(rotor_side, roll(value, HALO), roll(value, -HALO))

    def sector_of(n, by, holder, sign):
        base = by + sign * offset_ref[n] - 1 + 2 * n_azim
        sector = base + lax.rem(holder - lax.rem(base, GROUP) + GROUP, GROUP)
        return lax.rem(sector, n_azim) // GROUP

    def facing_of(n, d):
        offset = offset_ref[n]
        stator_from = lax.rem(me - offset - 1 + d + 2 * n_azim, GROUP)
        rotor_from = lax.rem(me + offset - 1 + d + 2 * n_azim, GROUP)
        return stator_from, rotor_from

    def relay(e, n):
        for i, peer in enumerate(near_peers):
            near_copy(e, peer, peer, i).wait_recv()
        near_held[...] = near[e]

        def chosen(peer):
            by = high * GROUP + peer
            return jnp.where(
                rotor_side[None], near_held[sector_of(n, by, low, -1)], near_held[sector_of(n, by, low, 1)]
            )

        for i, peer in enumerate(far_peers):
            far_send[e, i] = chosen(peer)
            far_copy(e, low, peer, i).start()
        far[e, low] = chosen(low)

    def relay_params():
        for i, peer in enumerate(near_peers):
            par_copy(peer, peer, i).wait_recv()

        def chosen(peer, n):
            by = high * GROUP + peer
            return jnp.where(
                rotor_side, par[sector_of(n, by, low, -1)], par[sector_of(n, by, low, 1)]
            )

        for i, peer in enumerate(far_peers):
            for n in range(steps):
                par_send[i, n] = chosen(peer, n)
            pfar_copy(low, peer, i).start()
        for n in range(steps):
            par_far[low, n] = chosen(low, n)

    def ghosts(e, n, tap):
        for i, peer in enumerate(far_peers):
            far_copy(e, peer, peer, i).wait_recv()
        far_held[...] = far[e]
        spots = [facing_of(n, d) for d in range(3)]
        out = []
        for f in range(fields):
            facing = [jnp.where(rotor_side, far_held[s, f], far_held[r, f]) for s, r in spots]
            out.append(blend(facing[0], facing[1], facing[2], tap))
        return out

    def merge(e):
        for f in range(fields):
            value = tile[e, f]
            for group in range(cells * r_tiles):
                a, t = group // r_tiles, group % r_tiles
                spot = roll(value, low_lane - RIM * group)
                cur[e, f, a, pl.ds(TILE * (t + 1), TILE), :] = jnp.where(
                    at_interface, spot, raw[e, f, a, TILE * t : TILE * (t + 1), :]
                )

    def axial_slopes(e):
        for f in range(fields):
            block = cur[e, f, :, rows, :].reshape(cells * radial, lanes)
            slopes[f] = dot(block, deriv[...]).reshape(cells, radial, lanes)
        out = []
        for f in range(fields):
            plain = packed(lambda a, t: slopes[f, a, TILE * t : TILE * (t + 1), :])
            out.append(plain - cross(tile[e, f]))
        return out

    def rim_state(e, base, scale, along):
        out = []
        slope = []
        for f in range(fields):
            here = tile[e, f]
            slope.append((
                along[f],
                radial_slope(side[e, 2, f], here, side[e, 3, f]),
                azim_slope(side[e, 0, f], here, side[e, 1, f]),
            ))
        spread = slope[1][0] + slope[2][1] + slope[3][2]
        forcing = (spread, slope[4][0], slope[4][1], slope[4][2], spread)
        for f in range(fields):
            advect = flow_pack[0] * slope[f][0] + flow_pack[1] * slope[f][1] + flow_pack[2] * slope[f][2]
            out.append(tile[base, f] - scale * (advect + forcing[f]))
        return out

    def bulk_local(e, base, scale):
        on_rad(lambda: rad_copy(e, 1).wait_recv(), lambda: rad_copy(e, 0).wait_recv())
        cur[e, :, :, pl.ds(TILE - HALO, HALO), :] = rad_halo[e, 0]
        cur[e, :, :, pl.ds(TILE + radial, HALO), :] = rad_halo[e, 1]
        for a in range(cells):
            along = []
            for f in range(fields):
                rad_slope = None
                for j in range(4):
                    term = STENCIL[j] * (
                        cur[e, f, a, pl.ds(TILE + j + 1, radial), :]
                        - cur[e, f, a, pl.ds(TILE - j - 1, radial), :]
                    )
                    rad_slope = term if rad_slope is None else rad_slope + term
                along.append((slopes[f, a], rad_slope))
            spread = along[1][0] + along[2][1]
            forcing = (spread, along[4][0], along[4][1], None, spread)
            for f in range(fields):
                total = flow_ref[0] * along[f][0] + flow_ref[1] * along[f][1]
                if forcing[f] is not None:
                    total = total + forcing[f]
                slopes[f, a] = cur[base, f, a, rows, :] - scale * total

    def bulk_azim(e, scale):
        for side_no in range(2):
            azim_copy(e, side_no).wait_recv()

        def cell_row(f, a):
            if a < 0:
                return azim_halo[e, 0, f, a + HALO]
            if a >= cells:
                return azim_halo[e, 1, f, a - cells]
            return cur[e, f, a, rows, :]

        for a in range(cells):
            along = []
            for f in range(fields):
                azim = None
                for j in range(4):
                    term = STENCIL[j] * (cell_row(f, a + j + 1) - cell_row(f, a - j - 1))
                    azim = term if azim is None else azim + term
                along.append(azim)
            forcing = (along[3], None, None, along[4], along[3])
            for f in range(fields):
                total = flow_ref[2] * along[f]
                if forcing[f] is not None:
                    total = total + forcing[f]
                raw[e + 1, f, a] = slopes[f, a] - scale * total

    half_step = 0.5 * STEP_SIZE

    def advance(n, carry):
        e = 2 * n
        n_row = n + 1
        tap = taps(
            per_lane(stator_fraction, rotor_fraction), per_lane(stator_first(n), rotor_first(n))
        )
        merge(e)
        along = axial_slopes(e)
        relay(e, n)
        wait_sides(e)
        midway = rim_state(e, e, half_step, along)
        for f in range(fields):
            near[e + 1, high, f] = midway[f]
        send_near(e + 1)
        bulk_local(e, e, half_step)

        @pl.when(n == 0)
        def _():
            relay_params()

        bulk_azim(e, half_step)
        send_halos(e + 1)
        push = across(ghosts(e, n, tap))
        for f in range(fields):
            tile[e + 1, f] = midway[f] - half_step * push[f]
        send_sides(e + 1)

        @pl.when(n == 0)
        def _():
            for i, peer in enumerate(far_peers):
                pfar_copy(peer, peer, i).wait_recv()

        merge(e + 1)
        along = axial_slopes(e + 1)

        other = []
        for d in range(3):
            stator_from, rotor_from = facing_of(n, d)
            there = jnp.where(rotor_side, par_far[stator_from, n], par_far[rotor_from, n])
            there = swapped(there)
            fraction = jnp.broadcast_to(there[0:1], shape)
            first = jnp.zeros(shape, jnp.float32)
            for i in range(steps):
                first = jnp.where(n == i, jnp.broadcast_to(there[i + 1 : i + 2], shape), first)
            other.append(taps(fraction, first))
        back = taps(
            per_lane(rotor_fraction, stator_fraction), per_lane(rotor_first(n), stator_first(n))
        )
        twice = []
        for f in range(fields):
            before, here, after = side[e, 0, f], tile[e, f], side[e, 1, f]
            twice.append(blend(
                blend(before, before, here, other[0]),
                blend(before, here, after, other[1]),
                blend(here, after, after, other[2]),
                back,
            ))
        mutual = across(twice)

        relay(e + 1, n)
        bulk_local(e + 1, e, STEP_SIZE)
        wait_sides(e + 1)
        final = rim_state(e + 1, e, STEP_SIZE, along)
        ghost = ghosts(e + 1, n, tap)
        push = across([ghost[f] - half_step * mutual[f] for f in range(fields)])
        for f in range(fields):
            tile[e + 2, f] = final[f] - STEP_SIZE * push[f]

        @pl.when(n + 1 < steps)
        def _():
            for f in range(fields):
                near[e + 2, high, f] = tile[e + 2, f]
            send_near(e + 2)
            send_sides(e + 2)

        bulk_azim(e + 1, STEP_SIZE)

        @pl.when(n + 1 < steps)
        def _():
            send_halos(e + 2)

        return carry

    lax.fori_loop(0, steps, advance, 0)
    for f in range(fields):
        value = tile[evals, f]
        for group in range(cells * r_tiles):
            a, t = group // r_tiles, group % r_tiles
            out_ref[f, a, TILE * t : TILE * (t + 1), :] = jnp.where(
                at_interface, roll(value, low_lane - RIM * group),
                raw[evals, f, a, TILE * t : TILE * (t + 1), :],
            )

    def finish(e, carry):
        for i, peer in enumerate(near_peers):
            near_copy(e, high, peer, i).wait_send()
        for i, peer in enumerate(far_peers):
            far_copy(e, low, peer, i).wait_send()
        for side_no in range(2):
            azim_copy(e, side_no).wait_send()
            side_copy(e, side_no).wait_send()

        def up():
            rad_copy(e, 0).wait_send()
            side_copy(e, 2).wait_send()

        def down():
            rad_copy(e, 1).wait_send()
            side_copy(e, 3).wait_send()

        on_rad(up, down)
        return carry

    lax.fori_loop(0, evals, finish, 0)
    for i, peer in enumerate(near_peers):
        par_copy(high, peer, i).wait_send()
    for i, peer in enumerate(far_peers):
        pfar_copy(low, peer, i).wait_send()


def solution(mesh):
    n_azim, n_rad = mesh.shape["azim"], mesh.shape["rad"]

    def shards(acoustic_state, mean_flow, sector_offset, cell_shift, stencil_start, interface_fraction):
        fields, cells, radial, lanes = acoustic_state.shape
        steps = sector_offset.shape[0]
        evals = 2 * steps
        n_high = n_azim // GROUP
        dims = (fields, cells, radial, lanes, steps, n_azim, n_rad)
        vmem = pl.BlockSpec(memory_space=pltpu.VMEM)
        f32 = jnp.float32
        dma = pltpu.SemaphoreType.DMA
        return pl.pallas_call(
            functools.partial(kernel, dims),
            out_shape=pltpu.VMEM(acoustic_state.shape, f32),
            in_specs=[pl.BlockSpec(memory_space=pl.ANY)] * 6,
            out_specs=vmem,
            scratch_shapes=[
                pltpu.VMEM(mean_flow.shape, f32),
                pltpu.SMEM(sector_offset.shape, jnp.int32),
                pltpu.SMEM(cell_shift.shape, jnp.int32),
                pltpu.SMEM(stencil_start.shape, jnp.int32),
                pltpu.SMEM(interface_fraction.shape, f32),
                dma((6,)),
                pltpu.VMEM((evals + 1, fields, cells, radial, lanes), f32),
                pltpu.VMEM((evals, fields, cells, radial + 2 * TILE, lanes), f32),
                pltpu.VMEM((evals, 2, fields, HALO, radial, lanes), f32),
                pltpu.VMEM((evals, 2, fields, cells, HALO, lanes), f32),
                pltpu.VMEM((evals, 2, fields, cells, HALO, lanes), f32),
                pltpu.VMEM((evals + 1, fields, TILE, lanes), f32),
                pltpu.VMEM((evals, 4, fields, TILE, lanes), f32),
                pltpu.VMEM((evals, n_high, fields, TILE, lanes), f32),
                pltpu.VMEM((evals, GROUP - 1, fields, TILE, lanes), f32),
                pltpu.VMEM((evals, GROUP, fields, TILE, lanes), f32),
                pltpu.VMEM((fields, cells, radial, lanes), f32),
                pltpu.VMEM((3, TILE, lanes), f32),
                pltpu.VMEM((lanes, lanes), f32),
                pltpu.VMEM((n_high, fields, TILE, lanes), f32),
                pltpu.VMEM((GROUP, fields, TILE, lanes), f32),
                pltpu.VMEM((n_high, TILE, lanes), f32),
                pltpu.VMEM((GROUP - 1, steps, TILE, lanes), f32),
                pltpu.VMEM((GROUP, steps, TILE, lanes), f32),
                dma((evals, n_high)), dma((evals, n_high)),
                dma((evals, GROUP)), dma((evals, GROUP)),
                dma((evals, 2)), dma((evals, 2)),
                dma((evals, 2)), dma((evals, 2)),
                dma((evals, 4)), dma((evals, 4)),
                dma((n_high,)), dma((n_high,)),
                dma((GROUP,)), dma((GROUP,)),
            ],
            compiler_params=pltpu.CompilerParams(collective_id=0, has_side_effects=True),
        )(acoustic_state, mean_flow, sector_offset, cell_shift, stencil_start, interface_fraction)

    return jax.shard_map(
        shards,
        mesh=mesh,
        in_specs=(
            P(None, "azim", "rad", None),
            P(None, "rad", None),
            P(),
            P(None, "azim"),
            P(None, "azim"),
            P(None, "azim"),
        ),
        out_specs=P(None, "azim", "rad", None),
        check_vma=False,
    )
```

time: 37.7 us -> 34.9 us (0.926)
  Pallas kernels: 36.8 us -> 34.1 us
    pallas_call x1, Pallas kernels: 36.8 us -> 34.1 us  [shards(): pl.pallas_call(functools.partial(kernel, dims), out_shape=pltpu.VMEM(acou...]
where the time goes in v2:
time: 34.9 us; the launch traced here: 34.8 us
  Pallas kernels  34.1 us (98%)
  local copies, waits for them, and re-layouts  0.73 us (2%)
    pallas_call x1, Pallas kernels, shards(): pl.pallas_call(functools.partial(kernel, dims), out_shape=pltpu.VMEM(acou...  34.1 us
    unnamed x1, local copies, waits for them, and re-layouts  0.73 us

profile of v2, /device:TPU:0, one launch (start us, length us, event | category | flops | bytes accessed | tf_op | source)
XLA Modules:
  0.0 34.8 jit_solution(8870965250835426026)
XLA Ops:
  0.0 34.1 %shard_map.64 = f32[5,8,16,128]{3,2,1,0:T(8,128)S(1)} custom-call(f32[5,8,16,128]{3,2,1,0:T(8,128)} %q_hbm.1, f32[3,16,128]{2,1,0:T(8,128)} %flow_hbm.1, s32[2]{0:T(128)} %offset_hbm.1, s32[2,8]{1,0:T(2,128)} %shift_hbm.1, s32[2,8]{1,0:T(2,128)} %start_hbm.1, f32[2,8]{1,0:T(2,128)} %fraction_hbm.1), custom_call_target="tpu_custom_call" | custom-call | tf_op jit(solution)/shard_map/pallas_call | solution.py:603
  34.1 0.7 %copy.8 = f32[5,8,16,128]{3,2,1,0:T(8,128)} copy(f32[5,8,16,128]{3,2,1,0:T(8,128)S(1)} %shard_map.64) | data formatting | bytes 655360

commit v3 on v2

--- a/solution.py
+++ b/solution.py
@@ -131,11 +131,14 @@
             device_id=(high * GROUP + peer, rad), device_id_type=MESH,
         )
 
-    def azim_copy(e, side_no):
+    cuts = (0, 3, 5)
+
+    def azim_copy(e, side_no, part):
         source = cells - HALO if side_no == 0 else 0
+        some = pl.ds(cuts[part], cuts[part + 1] - cuts[part])
         return pltpu.make_async_remote_copy(
-            src_ref=raw.at[e, :, pl.ds(source, HALO)], dst_ref=azim_halo.at[e, side_no],
-            send_sem=azim_ssem.at[e, side_no], recv_sem=azim_rsem.at[e, side_no],
+            src_ref=raw.at[e, some, pl.ds(source, HALO)], dst_ref=azim_halo.at[e, side_no, some],
+            send_sem=azim_ssem.at[e, side_no, part], recv_sem=azim_rsem.at[e, side_no, part],
             device_id=(right if side_no == 0 else left, rad), device_id_type=MESH,
         )
 
@@ -177,9 +180,12 @@
         side_copy(e, 0).wait_recv()
         side_copy(e, 1).wait_recv()
 
-    def send_halos(e):
-        for side_no in range(2):
-            azim_copy(e, side_no).start()
+    def send_halos(e, which):
+        for part in which:
+            for side_no in range(2):
+                azim_copy(e, side_no, part).start()
+        if 0 not in which:
+            return
 
         def up():
             rad_send[e, 0] = raw[e, :, :, pl.ds(radial - HALO, HALO), :]
@@ -226,7 +232,7 @@
 
     send_near(0)
     send_sides(0)
-    send_halos(0)
+    send_halos(0, range(2))
     for i, peer in enumerate(near_peers):
         par_copy(high, peer, i).start()
 
@@ -442,7 +448,8 @@
 
     def bulk_azim(e, scale):
         for side_no in range(2):
-            azim_copy(e, side_no).wait_recv()
+            for part in range(len(cuts) - 1):
+                azim_copy(e, side_no, part).wait_recv()
 
         def cell_row(f, a):
             if a < 0:
@@ -489,19 +496,22 @@
             relay_params()
 
         bulk_azim(e, half_step)
-        send_halos(e + 1)
+        send_halos(e + 1, (0,))
         push = across(ghosts(e, n, tap))
         for f in range(fields):
             tile[e + 1, f] = midway[f] - half_step * push[f]
         send_sides(e + 1)
 
+        merge(e + 1)
+        along = axial_slopes(e + 1)
+
+        relay(e + 1, n)
+        send_halos(e + 1, (1,))
+        bulk_local(e + 1, e, STEP_SIZE)
         @pl.when(n == 0)
         def _():
             for i, peer in enumerate(far_peers):
                 pfar_copy(peer, peer, i).wait_recv()
-
-        merge(e + 1)
-        along = axial_slopes(e + 1)
 
         other = []
         for d in range(3):
@@ -527,8 +537,6 @@
             ))
         mutual = across(twice)
 
-        relay(e + 1, n)
-        bulk_local(e + 1, e, STEP_SIZE)
         wait_sides(e + 1)
         final = rim_state(e + 1, e, STEP_SIZE, along)
         ghost = ghosts(e + 1, n, tap)
@@ -547,7 +555,7 @@
 
         @pl.when(n + 1 < steps)
         def _():
-            send_halos(e + 2)
+            send_halos(e + 2, range(2))
 
         return carry
 
@@ -567,7 +575,8 @@
         for i, peer in enumerate(far_peers):
             far_copy(e, low, peer, i).wait_send()
         for side_no in range(2):
-            azim_copy(e, side_no).wait_send()
+            for part in range(len(cuts) - 1):
+                azim_copy(e, side_no, part).wait_send()
             side_copy(e, side_no).wait_send()
 
         def up():
@@ -632,7 +641,7 @@
                 pltpu.VMEM((GROUP, steps, TILE, lanes), f32),
                 dma((evals, n_high)), dma((evals, n_high)),
                 dma((evals, GROUP)), dma((evals, GROUP)),
-                dma((evals, 2)), dma((evals, 2)),
+                dma((evals, 2, 2)), dma((evals, 2, 2)),
                 dma((evals, 2)), dma((evals, 2)),
                 dma((evals, 4)), dma((evals, 4)),
                 dma((n_high,)), dma((n_high,)),

time: 34.9 us -> 34 us (0.974)
  Pallas kernels: 34.1 us -> 33.2 us
    pallas_call x1, Pallas kernels: 34.1 us -> 33.2 us  [shards(): pl.pallas_call(functools.partial(kernel, dims), out_shape=pltpu.VMEM(acou...]
where the time goes in v3:
time: 34 us; the launch traced here: 33.9 us
  Pallas kernels  33.2 us (98%)
  local copies, waits for them, and re-layouts  0.73 us (2%)
    pallas_call x1, Pallas kernels, shards(): pl.pallas_call(functools.partial(kernel, dims), out_shape=pltpu.VMEM(acou...  33.2 us
    unnamed x1, local copies, waits for them, and re-layouts  0.73 us

profile of v3, /device:TPU:0, one launch (start us, length us, event | category | flops | bytes accessed | tf_op | source)
XLA Modules:
  0.0 33.9 jit_solution(16057833108802118355)
XLA Ops:
  0.0 33.2 %shard_map.64 = f32[5,8,16,128]{3,2,1,0:T(8,128)S(1)} custom-call(f32[5,8,16,128]{3,2,1,0:T(8,128)} %q_hbm.1, f32[3,16,128]{2,1,0:T(8,128)} %flow_hbm.1, s32[2]{0:T(128)} %offset_hbm.1, s32[2,8]{1,0:T(2,128)} %shift_hbm.1, s32[2,8]{1,0:T(2,128)} %start_hbm.1, f32[2,8]{1,0:T(2,128)} %fraction_hbm.1), custom_call_target="tpu_custom_call" | custom-call | tf_op jit(solution)/shard_map/pallas_call | solution.py:612
  33.2 0.7 %copy.8 = f32[5,8,16,128]{3,2,1,0:T(8,128)} copy(f32[5,8,16,128]{3,2,1,0:T(8,128)S(1)} %shard_map.64) | data formatting | bytes 655360

commit v4 on v3

--- a/solution.py
+++ b/solution.py
@@ -446,7 +446,7 @@
                     total = total + forcing[f]
                 slopes[f, a] = cur[base, f, a, rows, :] - scale * total
 
-    def bulk_azim(e, scale):
+    def bulk_azim(e, scale, put):
         for side_no in range(2):
             for part in range(len(cuts) - 1):
                 azim_copy(e, side_no, part).wait_recv()
@@ -471,7 +471,19 @@
                 total = flow_ref[2] * along[f]
                 if forcing[f] is not None:
                     total = total + forcing[f]
-                raw[e + 1, f, a] = slopes[f, a] - scale * total
+                put(f, a, slopes[f, a] - scale * total)
+
+    def keep(e):
+        def put(f, a, value):
+            raw[e, f, a] = value
+
+        return put
+
+    def give(f, a, value):
+        for t in range(r_tiles):
+            part = slice(TILE * t, TILE * (t + 1))
+            spot = roll(tile[evals, f], low_lane - RIM * (a * r_tiles + t))
+            out_ref[f, a, part, :] = jnp.where(at_interface, spot, value[part])
 
     half_step = 0.5 * STEP_SIZE
 
@@ -495,7 +507,7 @@
         def _():
             relay_params()
 
-        bulk_azim(e, half_step)
+        bulk_azim(e, half_step, keep(e + 1))
         send_halos(e + 1, (0,))
         push = across(ghosts(e, n, tap))
         for f in range(fields):
@@ -551,24 +563,18 @@
             send_near(e + 2)
             send_sides(e + 2)
 
-        bulk_azim(e + 1, STEP_SIZE)
-
         @pl.when(n + 1 < steps)
         def _():
+            bulk_azim(e + 1, STEP_SIZE, keep(e + 2))
             send_halos(e + 2, range(2))
 
+        @pl.when(n + 1 == steps)
+        def _():
+            bulk_azim(e + 1, STEP_SIZE, give)
+
         return carry
 
     lax.fori_loop(0, steps, advance, 0)
-    for f in range(fields):
-        value = tile[evals, f]
-        for group in range(cells * r_tiles):
-            a, t = group // r_tiles, group % r_tiles
-            out_ref[f, a, TILE * t : TILE * (t + 1), :] = jnp.where(
-                at_interface, roll(value, low_lane - RIM * group),
-                raw[evals, f, a, TILE * t : TILE * (t + 1), :],
-            )
-
     def finish(e, carry):
         for i, peer in enumerate(near_peers):
             near_copy(e, high, peer, i).wait_send()

time: 34 us -> 33.9 us (level)
  no operation moved by 1% of the time
where the time goes in v4:
time: 33.9 us; the launch traced here: 33.8 us
  Pallas kernels  33 us (97%)
  local copies, waits for them, and re-layouts  0.73 us (2%)
    pallas_call x1, Pallas kernels, shards(): pl.pallas_call(functools.partial(kernel, dims), out_shape=pltpu.VMEM(acou...  33 us
    unnamed x1, local copies, waits for them, and re-layouts  0.73 us

profile of v4, /device:TPU:0, one launch (start us, length us, event | category | flops | bytes accessed | tf_op | source)
XLA Modules:
  0.0 33.8 jit_solution(16503761607427791582)
XLA Ops:
  0.0 33.0 %shard_map.64 = f32[5,8,16,128]{3,2,1,0:T(8,128)S(1)} custom-call(f32[5,8,16,128]{3,2,1,0:T(8,128)} %q_hbm.1, f32[3,16,128]{2,1,0:T(8,128)} %flow_hbm.1, s32[2]{0:T(128)} %offset_hbm.1, s32[2,8]{1,0:T(2,128)} %shift_hbm.1, s32[2,8]{1,0:T(2,128)} %start_hbm.1, f32[2,8]{1,0:T(2,128)} %fraction_hbm.1), custom_call_target="tpu_custom_call" | custom-call | tf_op jit(solution)/shard_map/pallas_call | solution.py:618
  33.0 0.7 %copy.8 = f32[5,8,16,128]{3,2,1,0:T(8,128)} copy(f32[5,8,16,128]{3,2,1,0:T(8,128)S(1)} %shard_map.64) | data formatting | bytes 655360

commit v5 on v4

--- a/solution.py
+++ b/solution.py
@@ -46,7 +46,8 @@
     rad = lax.axis_index("rad")
     high, low = me // GROUP, lax.rem(me, GROUP)
     left, right = lax.rem(me + n_azim - 1, n_azim), lax.rem(me + 1, n_azim)
-    near_peers = [lax.rem(high + i, n_high) for i in range(1, n_high)]
+    turn = 2 * (high // ((n_high + 1) // 2)) - 1
+    near_peers = [lax.rem(high + turn * i + n_high, n_high) for i in range(1, n_high)]
     far_peers = [lax.rem(low + i, GROUP) for i in range(1, GROUP)]
 
     rows = pl.ds(TILE, radial)

time: 33.9 us -> 34.4 us (1.015)
  Pallas kernels: 33 us -> 33.5 us
    pallas_call x1, Pallas kernels: 33 us -> 33.5 us  [shards(): pl.pallas_call(functools.partial(kernel, dims), out_shape=pltpu.VMEM(acou...]
where the time goes in v5:
time: 34.4 us; the launch traced here: 34.2 us
  Pallas kernels  33.5 us (97%)
  local copies, waits for them, and re-layouts  0.73 us (2%)
    pallas_call x1, Pallas kernels, shards(): pl.pallas_call(functools.partial(kernel, dims), out_shape=pltpu.VMEM(acou...  33.5 us
    unnamed x1, local copies, waits for them, and re-layouts  0.73 us

profile of v5, /device:TPU:0, one launch (start us, length us, event | category | flops | bytes accessed | tf_op | source)
XLA Modules:
  0.0 34.2 jit_solution(15399792569531336495)
XLA Ops:
  0.0 33.5 %shard_map.64 = f32[5,8,16,128]{3,2,1,0:T(8,128)S(1)} custom-call(f32[5,8,16,128]{3,2,1,0:T(8,128)} %q_hbm.1, f32[3,16,128]{2,1,0:T(8,128)} %flow_hbm.1, s32[2]{0:T(128)} %offset_hbm.1, s32[2,8]{1,0:T(2,128)} %shift_hbm.1, s32[2,8]{1,0:T(2,128)} %start_hbm.1, f32[2,8]{1,0:T(2,128)} %fraction_hbm.1), custom_call_target="tpu_custom_call" | custom-call | tf_op jit(solution)/shard_map/pallas_call | solution.py:619
  33.5 0.7 %copy.8 = f32[5,8,16,128]{3,2,1,0:T(8,128)} copy(f32[5,8,16,128]{3,2,1,0:T(8,128)S(1)} %shard_map.64) | data formatting | bytes 655360
